TPU v7x, 32 devices: a 4x2x2 block of a 4x4x8 slice. The times are simulated.
32 devices in a mesh: parts: 4 (over y, z), data: 8 (over x, core).
Axes of the slice: x: 4, y: 2, z: 2, core: 2. Of those that a mesh axis runs over, the one named last changes fastest.
The devices are a block of a 4x4x8 slice.
Arguments:
- features: bfloat16 [16384, 1536], P('data')
- labels: int32 [16384], P('data')
- theta_start: float32 [1536, 8], P(None, 'parts'), parts along dimension 1
- momentum_start: float32 [1536, 8], P(None, 'parts'), parts along dimension 1
Outputs:
- output 1: float32 [1536, 8], P(None, 'parts'), parts along dimension 1
- output 2: float32 [1536, 8], P(None, 'parts'), parts along dimension 1
- output 3: float32 [8], P('parts'), parts along dimension 0
There are 4 independent parts. A program takes and returns all parts, laid end to end along the dimension named above; an argument that names none is the same for every part.
All inputs are finite; a program needn't handle non-finite values.
Results may differ from a plain program's by a relative error of at most 0.00262983.
Values are sent between devices in bfloat16 or wider.
A program may use at most 768 MiB of HBM per device.

v0:
```python
import math
import jax
import jax.numpy as jnp
from jax import lax
from jax.sharding import PartitionSpec as P, NamedSharding

LEAPFROG = 32
PRIOR_VAR = 1.0
STEP_COEF = 0.3


def solution(mesh):
    data_size = mesh.shape['data']

    def local_run(feat_loc, label_loc, theta_start, momentum_start):
        rows_loc, feat_dim = feat_loc.shape
        step_size = STEP_COEF * math.sqrt(feat_dim / (rows_loc * data_size))
        label_col = label_loc.astype(jnp.float32)[:, None]

        def grad_fn(position):
            logits = jnp.dot(feat_loc, position.astype(jnp.bfloat16), preferred_element_type=jnp.float32)
            residual = (label_col - jax.nn.sigmoid(logits)).astype(jnp.bfloat16)
            part_grad = lax.dot_general(feat_loc, residual, (((0,), (0,)), ((), ())), preferred_element_type=jnp.float32)
            full_grad = lax.psum(part_grad, 'data')
            return full_grad - position / PRIOR_VAR, logits

        grad_val, _ = grad_fn(theta_start)
        momentum = momentum_start + 0.5 * step_size * grad_val

        def loop_body(step_index, carry):
            position, moment_cur = carry
            position = position + step_size * moment_cur
            grad_cur, _ = grad_fn(position)
            return position, moment_cur + step_size * grad_cur

        position, momentum = lax.fori_loop(0, LEAPFROG - 1, loop_body, (theta_start, momentum))
        position = position + step_size * momentum
        grad_val, logits = grad_fn(position)
        momentum = momentum + 0.5 * step_size * grad_val
        row_terms = jnp.sum(jax.nn.softplus(logits) - label_col * logits, axis=0)
        potential = lax.psum(row_terms, 'data') + jnp.sum(position * position, axis=0) / (2.0 * PRIOR_VAR)
        energy = potential + 0.5 * jnp.sum(momentum * momentum, axis=0)
        return position, momentum, energy

    return jax.shard_map(local_run, mesh=mesh, in_specs=(P('data', None), P('data'), P(None, 'parts'), P(None, 'parts')), out_specs=(P(None, 'parts'), P(None, 'parts'), P('parts')), check_vma=False)
```

profile of v0, /device:TPU:88, one launch (start us, length us, event | category | flops | bytes accessed | tf_op | source)
XLA Modules:
  0.0 1030.8 jit_solution(15216692243084409069)
XLA Ops:
  9.5 26.1 %psum.28 = f32[1536,2]{0,1:T(2,128)S(1)} all-reduce(f32[1536,2]{0,1:T(2,128)S(1)} %convolution_bitcast_fusion.3), channel_id=1, replica_groups=mesh['parts'=4,'data'=8] {'data'}, use_global_device_ids=true, to_apply=%region_0.0 | all-reduce | flops 3072 | bytes 24576 | tf_op jit(solution)/shard_map/psum | solution.py:24
  35.6 964.4 %while.12 = (s32[]{:T(128)}, f32[1536,2]{0,1:T(2,128)S(1)}, f32[1536,2]{0,1:T(2,128)S(1)}, f32[2048,1]{0,1:T(1,128)S(1)}, bf16[2048,1536]{1,0:T(8,128)(2,1)}, /*index=5*/s32[]{:T(128)}) while((s32[]{:T(128)}, f32[1536,2]{0,1:T(2,128)S(1)}, f32[1536,2]{0,1:T(2,128)S(1)}, f32[2048,1]{0,1:T(1,128)S(1)}, bf16[2048,1536]{1,0:T(8,128)(2,1)}, ...), condition=%wide.region_3.0_spmd, body=%wide.region_1.0_spmd.sunk | while | flops 25207808 | bytes 6434885 | solution.py:36
  35.6 7.4 convolution_bitcast_fusion.5
  43.1 23.6 %psum.32 = f32[1536,2]{0,1:T(2,128)S(1)} all-reduce(f32[1536,2]{0,1:T(2,128)S(1)} %convolution_bitcast_fusion.5), channel_id=1, replica_groups=mesh['parts'=4,'data'=8] {'data'}, use_global_device_ids=true, to_apply=%region_2.0 | all-reduce | flops 3072 | bytes 24576 | tf_op jit(solution)/shard_map/while/body/eval_jaxpr/psum | solution.py:24
  66.7 7.4 convolution_bitcast_fusion.5
  74.2 23.6 %psum.32 = f32[1536,2]{0,1:T(2,128)S(1)} all-reduce(f32[1536,2]{0,1:T(2,128)S(1)} %convolution_bitcast_fusion.5), channel_id=1, replica_groups=mesh['parts'=4,'data'=8] {'data'}, use_global_device_ids=true, to_apply=%region_2.0 | all-reduce | flops 3072 | bytes 24576 | tf_op jit(solution)/shard_map/while/body/eval_jaxpr/psum | solution.py:24
  97.9 7.4 convolution_bitcast_fusion.5
  105.3 23.6 %psum.32 = f32[1536,2]{0,1:T(2,128)S(1)} all-reduce(f32[1536,2]{0,1:T(2,128)S(1)} %convolution_bitcast_fusion.5), channel_id=1, replica_groups=mesh['parts'=4,'data'=8] {'data'}, use_global_device_ids=true, to_apply=%region_2.0 | all-reduce | flops 3072 | bytes 24576 | tf_op jit(solution)/shard_map/while/body/eval_jaxpr/psum | solution.py:24
  129.0 7.4 convolution_bitcast_fusion.5
  136.4 23.6 %psum.32 = f32[1536,2]{0,1:T(2,128)S(1)} all-reduce(f32[1536,2]{0,1:T(2,128)S(1)} %convolution_bitcast_fusion.5), channel_id=1, replica_groups=mesh['parts'=4,'data'=8] {'data'}, use_global_device_ids=true, to_apply=%region_2.0 | all-reduce | flops 3072 | bytes 24576 | tf_op jit(solution)/shard_map/while/body/eval_jaxpr/psum | solution.py:24
  160.1 7.4 convolution_bitcast_fusion.5
  167.5 23.6 %psum.32 = f32[1536,2]{0,1:T(2,128)S(1)} all-reduce(f32[1536,2]{0,1:T(2,128)S(1)} %convolution_bitcast_fusion.5), channel_id=1, replica_groups=mesh['parts'=4,'data'=8] {'data'}, use_global_device_ids=true, to_apply=%region_2.0 | all-reduce | flops 3072 | bytes 24576 | tf_op jit(solution)/shard_map/while/body/eval_jaxpr/psum | solution.py:24
  191.2 7.4 convolution_bitcast_fusion.5
  198.6 23.6 %psum.32 = f32[1536,2]{0,1:T(2,128)S(1)} all-reduce(f32[1536,2]{0,1:T(2,128)S(1)} %convolution_bitcast_fusion.5), channel_id=1, replica_groups=mesh['parts'=4,'data'=8] {'data'}, use_global_device_ids=true, to_apply=%region_2.0 | all-reduce | flops 3072 | bytes 24576 | tf_op jit(solution)/shard_map/while/body/eval_jaxpr/psum | solution.py:24
  222.3 7.4 convolution_bitcast_fusion.5
  229.7 23.6 %psum.32 = f32[1536,2]{0,1:T(2,128)S(1)} all-reduce(f32[1536,2]{0,1:T(2,128)S(1)} %convolution_bitcast_fusion.5), channel_id=1, replica_groups=mesh['parts'=4,'data'=8] {'data'}, use_global_device_ids=true, to_apply=%region_2.0 | all-reduce | flops 3072 | bytes 24576 | tf_op jit(solution)/shard_map/while/body/eval_jaxpr/psum | solution.py:24
  253.4 7.4 convolution_bitcast_fusion.5
  260.9 23.6 %psum.32 = f32[1536,2]{0,1:T(2,128)S(1)} all-reduce(f32[1536,2]{0,1:T(2,128)S(1)} %convolution_bitcast_fusion.5), channel_id=1, replica_groups=mesh['parts'=4,'data'=8] {'data'}, use_global_device_ids=true, to_apply=%region_2.0 | all-reduce | flops 3072 | bytes 24576 | tf_op jit(solution)/shard_map/while/body/eval_jaxpr/psum | solution.py:24
  284.5 7.4 convolution_bitcast_fusion.5
  292.0 23.6 %psum.32 = f32[1536,2]{0,1:T(2,128)S(1)} all-reduce(f32[1536,2]{0,1:T(2,128)S(1)} %convolution_bitcast_fusion.5), channel_id=1, replica_groups=mesh['parts'=4,'data'=8] {'data'}, use_global_device_ids=true, to_apply=%region_2.0 | all-reduce | flops 3072 | bytes 24576 | tf_op jit(solution)/shard_map/while/body/eval_jaxpr/psum | solution.py:24
  315.6 7.4 convolution_bitcast_fusion.5
  323.1 23.6 %psum.32 = f32[1536,2]{0,1:T(2,128)S(1)} all-reduce(f32[1536,2]{0,1:T(2,128)S(1)} %convolution_bitcast_fusion.5), channel_id=1, replica_groups=mesh['parts'=4,'data'=8] {'data'}, use_global_device_ids=true, to_apply=%region_2.0 | all-reduce | flops 3072 | bytes 24576 | tf_op jit(solution)/shard_map/while/body/eval_jaxpr/psum | solution.py:24
  346.7 7.4 convolution_bitcast_fusion.5
  354.2 23.6 %psum.32 = f32[1536,2]{0,1:T(2,128)S(1)} all-reduce(f32[1536,2]{0,1:T(2,128)S(1)} %convolution_bitcast_fusion.5), channel_id=1, replica_groups=mesh['parts'=4,'data'=8] {'data'}, use_global_device_ids=true, to_apply=%region_2.0 | all-reduce | flops 3072 | bytes 24576 | tf_op jit(solution)/shard_map/while/body/eval_jaxpr/psum | solution.py:24
  377.8 7.4 convolution_bitcast_fusion.5
  385.3 23.6 %psum.32 = f32[1536,2]{0,1:T(2,128)S(1)} all-reduce(f32[1536,2]{0,1:T(2,128)S(1)} %convolution_bitcast_fusion.5), channel_id=1, replica_groups=mesh['parts'=4,'data'=8] {'data'}, use_global_device_ids=true, to_apply=%region_2.0 | all-reduce | flops 3072 | bytes 24576 | tf_op jit(solution)/shard_map/while/body/eval_jaxpr/psum | solution.py:24
  409.0 7.4 convolution_bitcast_fusion.5
  416.4 23.6 %psum.32 = f32[1536,2]{0,1:T(2,128)S(1)} all-reduce(f32[1536,2]{0,1:T(2,128)S(1)} %convolution_bitcast_fusion.5), channel_id=1, replica_groups=mesh['parts'=4,'data'=8] {'data'}, use_global_device_ids=true, to_apply=%region_2.0 | all-reduce | flops 3072 | bytes 24576 | tf_op jit(solution)/shard_map/while/body/eval_jaxpr/psum | solution.py:24
  440.1 7.4 convolution_bitcast_fusion.5
  447.5 23.6 %psum.32 = f32[1536,2]{0,1:T(2,128)S(1)} all-reduce(f32[1536,2]{0,1:T(2,128)S(1)} %convolution_bitcast_fusion.5), channel_id=1, replica_groups=mesh['parts'=4,'data'=8] {'data'}, use_global_device_ids=true, to_apply=%region_2.0 | all-reduce | flops 3072 | bytes 24576 | tf_op jit(solution)/shard_map/while/body/eval_jaxpr/psum | solution.py:24
  478.6 23.6 %psum.32 = f32[1536,2]{0,1:T(2,128)S(1)} all-reduce(f32[1536,2]{0,1:T(2,128)S(1)} %convolution_bitcast_fusion.5), channel_id=1, replica_groups=mesh['parts'=4,'data'=8] {'data'}, use_global_device_ids=true, to_apply=%region_2.0 | all-reduce | flops 3072 | bytes 24576 | tf_op jit(solution)/shard_map/while/body/eval_jaxpr/psum | solution.py:24
  509.7 23.6 %psum.32 = f32[1536,2]{0,1:T(2,128)S(1)} all-reduce(f32[1536,2]{0,1:T(2,128)S(1)} %convolution_bitcast_fusion.5), channel_id=1, replica_groups=mesh['parts'=4,'data'=8] {'data'}, use_global_device_ids=true, to_apply=%region_2.0 | all-reduce | flops 3072 | bytes 24576 | tf_op jit(solution)/shard_map/while/body/eval_jaxpr/psum | solution.py:24
  540.8 23.6 %psum.32 = f32[1536,2]{0,1:T(2,128)S(1)} all-reduce(f32[1536,2]{0,1:T(2,128)S(1)} %convolution_bitcast_fusion.5), channel_id=1, replica_groups=mesh['parts'=4,'data'=8] {'data'}, use_global_device_ids=true, to_apply=%region_2.0 | all-reduce | flops 3072 | bytes 24576 | tf_op jit(solution)/shard_map/while/body/eval_jaxpr/psum | solution.py:24
  572.0 23.6 %psum.32 = f32[1536,2]{0,1:T(2,128)S(1)} all-reduce(f32[1536,2]{0,1:T(2,128)S(1)} %convolution_bitcast_fusion.5), channel_id=1, replica_groups=mesh['parts'=4,'data'=8] {'data'}, use_global_device_ids=true, to_apply=%region_2.0 | all-reduce | flops 3072 | bytes 24576 | tf_op jit(solution)/shard_map/while/body/eval_jaxpr/psum | solution.py:24
  603.1 23.6 %psum.32 = f32[1536,2]{0,1:T(2,128)S(1)} all-reduce(f32[1536,2]{0,1:T(2,128)S(1)} %convolution_bitcast_fusion.5), channel_id=1, replica_groups=mesh['parts'=4,'data'=8] {'data'}, use_global_device_ids=true, to_apply=%region_2.0 | all-reduce | flops 3072 | bytes 24576 | tf_op jit(solution)/shard_map/while/body/eval_jaxpr/psum | solution.py:24
  634.2 23.6 %psum.32 = f32[1536,2]{0,1:T(2,128)S(1)} all-reduce(f32[1536,2]{0,1:T(2,128)S(1)} %convolution_bitcast_fusion.5), channel_id=1, replica_groups=mesh['parts'=4,'data'=8] {'data'}, use_global_device_ids=true, to_apply=%region_2.0 | all-reduce | flops 3072 | bytes 24576 | tf_op jit(solution)/shard_map/while/body/eval_jaxpr/psum | solution.py:24
  665.3 23.6 %psum.32 = f32[1536,2]{0,1:T(2,128)S(1)} all-reduce(f32[1536,2]{0,1:T(2,128)S(1)} %convolution_bitcast_fusion.5), channel_id=1, replica_groups=mesh['parts'=4,'data'=8] {'data'}, use_global_device_ids=true, to_apply=%region_2.0 | all-reduce | flops 3072 | bytes 24576 | tf_op jit(solution)/shard_map/while/body/eval_jaxpr/psum | solution.py:24
  696.4 23.6 %psum.32 = f32[1536,2]{0,1:T(2,128)S(1)} all-reduce(f32[1536,2]{0,1:T(2,128)S(1)} %convolution_bitcast_fusion.5), channel_id=1, replica_groups=mesh['parts'=4,'data'=8] {'data'}, use_global_device_ids=true, to_apply=%region_2.0 | all-reduce | flops 3072 | bytes 24576 | tf_op jit(solution)/shard_map/while/body/eval_jaxpr/psum | solution.py:24
  727.5 23.6 %psum.32 = f32[1536,2]{0,1:T(2,128)S(1)} all-reduce(f32[1536,2]{0,1:T(2,128)S(1)} %convolution_bitcast_fusion.5), channel_id=1, replica_groups=mesh['parts'=4,'data'=8] {'data'}, use_global_device_ids=true, to_apply=%region_2.0 | all-reduce | flops 3072 | bytes 24576 | tf_op jit(solution)/shard_map/while/body/eval_jaxpr/psum | solution.py:24
  758.6 23.6 %psum.32 = f32[1536,2]{0,1:T(2,128)S(1)} all-reduce(f32[1536,2]{0,1:T(2,128)S(1)} %convolution_bitcast_fusion.5), channel_id=1, replica_groups=mesh['parts'=4,'data'=8] {'data'}, use_global_device_ids=true, to_apply=%region_2.0 | all-reduce | flops 3072 | bytes 24576 | tf_op jit(solution)/shard_map/while/body/eval_jaxpr/psum | solution.py:24
  789.7 23.6 %psum.32 = f32[1536,2]{0,1:T(2,128)S(1)} all-reduce(f32[1536,2]{0,1:T(2,128)S(1)} %convolution_bitcast_fusion.5), channel_id=1, replica_groups=mesh['parts'=4,'data'=8] {'data'}, use_global_device_ids=true, to_apply=%region_2.0 | all-reduce | flops 3072 | bytes 24576 | tf_op jit(solution)/shard_map/while/body/eval_jaxpr/psum | solution.py:24
  820.8 23.6 %psum.32 = f32[1536,2]{0,1:T(2,128)S(1)} all-reduce(f32[1536,2]{0,1:T(2,128)S(1)} %convolution_bitcast_fusion.5), channel_id=1, replica_groups=mesh['parts'=4,'data'=8] {'data'}, use_global_device_ids=true, to_apply=%region_2.0 | all-reduce | flops 3072 | bytes 24576 | tf_op jit(solution)/shard_map/while/body/eval_jaxpr/psum | solution.py:24
  851.9 23.6 %psum.32 = f32[1536,2]{0,1:T(2,128)S(1)} all-reduce(f32[1536,2]{0,1:T(2,128)S(1)} %convolution_bitcast_fusion.5), channel_id=1, replica_groups=mesh['parts'=4,'data'=8] {'data'}, use_global_device_ids=true, to_apply=%region_2.0 | all-reduce | flops 3072 | bytes 24576 | tf_op jit(solution)/shard_map/while/body/eval_jaxpr/psum | solution.py:24
  883.1 23.6 %psum.32 = f32[1536,2]{0,1:T(2,128)S(1)} all-reduce(f32[1536,2]{0,1:T(2,128)S(1)} %convolution_bitcast_fusion.5), channel_id=1, replica_groups=mesh['parts'=4,'data'=8] {'data'}, use_global_device_ids=true, to_apply=%region_2.0 | all-reduce | flops 3072 | bytes 24576 | tf_op jit(solution)/shard_map/while/body/eval_jaxpr/psum | solution.py:24
  914.2 23.6 %psum.32 = f32[1536,2]{0,1:T(2,128)S(1)} all-reduce(f32[1536,2]{0,1:T(2,128)S(1)} %convolution_bitcast_fusion.5), channel_id=1, replica_groups=mesh['parts'=4,'data'=8] {'data'}, use_global_device_ids=true, to_apply=%region_2.0 | all-reduce | flops 3072 | bytes 24576 | tf_op jit(solution)/shard_map/while/body/eval_jaxpr/psum | solution.py:24
  945.3 23.6 %psum.32 = f32[1536,2]{0,1:T(2,128)S(1)} all-reduce(f32[1536,2]{0,1:T(2,128)S(1)} %convolution_bitcast_fusion.5), channel_id=1, replica_groups=mesh['parts'=4,'data'=8] {'data'}, use_global_device_ids=true, to_apply=%region_2.0 | all-reduce | flops 3072 | bytes 24576 | tf_op jit(solution)/shard_map/while/body/eval_jaxpr/psum | solution.py:24
  976.4 23.6 %psum.32 = f32[1536,2]{0,1:T(2,128)S(1)} all-reduce(f32[1536,2]{0,1:T(2,128)S(1)} %convolution_bitcast_fusion.5), channel_id=1, replica_groups=mesh['parts'=4,'data'=8] {'data'}, use_global_device_ids=true, to_apply=%region_2.0 | all-reduce | flops 3072 | bytes 24576 | tf_op jit(solution)/shard_map/while/body/eval_jaxpr/psum | solution.py:24
  1005.9 23.6 %all-reduce = (f32[1536,2]{0,1:T(2,128)S(1)}, f32[2]{0:T(128)S(1)}) all-reduce(f32[1536,2]{0,1:T(2,128)S(1)} %convolution_bitcast_fusion.2, f32[2]{0:T(128)S(1)} %get-tuple-element.49), channel_id=1, replica_groups=mesh['parts'=4,'data'=8] {'data'}, use_global_device_ids=true, to_apply=%region_4.0 | all-reduce | flops 3074 | bytes 24592 | tf_op jit(solution)/shard_map/psum | solution.py:24
  (94 shorter events, 143.8 us)
Async XLA Ops:
  2.0 33.5 %copy-start.2 = (f32[1536,2]{0,1:T(2,128)S(1)}, f32[1536,2]{0,1:T(2,128)}, u32[]{:S(2)}) copy-start(f32[1536,2]{0,1:T(2,128)} %param.9) | copy-start | bytes 36868
  1000.0 4.9 copy-start
  1000.2 29.4 %copy-start.1 = (f32[1536,2]{0,1:T(2,128)}, f32[1536,2]{0,1:T(2,128)S(1)}, u32[]{:S(2)}) copy-start(f32[1536,2]{0,1:T(2,128)S(1)} %get-tuple-element.46) | copy-start | bytes 36868
where the time goes:
time: 1030 us
  blocking collectives  782 us (76%)
  matrix products  244 us (24%)
    psum x33, blocking collectives, grad_fn(): full_grad = lax.psum(part_grad, 'data')  782 us
    dot_general x33, matrix products, grad_fn(): lax.dot_general(feat_loc, residual, (((0,), (0,)), ((), ())), preferred_e...  239 us

commit v1 on v0

v1 whole, which is shorter than its diff:
```python
import functools
import math
import jax
import jax.numpy as jnp
from jax import lax
from jax.experimental import pallas as pl
from jax.experimental.pallas import tpu as pltpu
from jax.sharding import PartitionSpec as P

LEAPFROG = 32
PRIOR_VAR = 1.0
STEP_COEF = 0.3
CHUNK = 512
TILE = 256


def trajectory(n, step_size, feat_hbm, label_ref, theta0_ref, mom0_ref,
               theta_out, mom_out, energy_out,
               feat, feat_t, logits_ref, theta_ref, mom_ref, buf, ebuf,
               load_sem, send_sem, recv_sem, esend_sem, erecv_sem):
    rows, dim = feat.shape
    chains = theta0_ref.shape[0]
    chunks = dim // CHUNK
    row_tiles = rows // TILE
    me = lax.axis_index('data')
    chip, core = me // 2, me % 2
    chips = n // 2
    hops = sorted(range(chips), key=lambda d: -min(d, chips - d))
    peers = [lax.rem(chip + d, chips) * 2 + (lax.rem(core + c, 2)) for d in hops for c in (0, 1) if (d, c) != (0, 0)]

    loads = []
    for t in range(row_tiles):
        copy = pltpu.make_async_copy(feat_hbm.at[pl.ds(t * TILE, TILE), :], feat.at[pl.ds(t * TILE, TILE), :], load_sem.at[t])
        copy.start()
        loads.append(copy)

    barrier = pltpu.get_barrier_semaphore()
    for peer in peers:
        pl.semaphore_signal(barrier, inc=1, device_id={'data': peer}, device_id_type=pl.DeviceIdType.MESH)

    theta_ref[...] = theta0_ref[...]
    mom_ref[...] = mom0_ref[...]

    def lhs(v):
        return jnp.concatenate([v, jnp.zeros((8 - chains, v.shape[1]), jnp.float32)], axis=0).astype(jnp.bfloat16)

    theta16 = lhs(theta0_ref[...])
    for t in range(row_tiles):
        loads[t].wait()
        for c in range(dim // TILE):
            feat_t[c * TILE:(c + 1) * TILE, t * TILE:(t + 1) * TILE] = feat[t * TILE:(t + 1) * TILE, c * TILE:(c + 1) * TILE].T
        logits_ref[:, t * TILE:(t + 1) * TILE] = jnp.dot(theta16, feat_t[:, t * TILE:(t + 1) * TILE], preferred_element_type=jnp.float32)

    pl.semaphore_wait(barrier, n - 1)

    def evaluate(step, last):
        par = lax.rem(step, 2)
        label_row = label_ref[...].astype(jnp.float32)
        logits = logits_ref[...]
        if last:
            z = logits[:chains]
            terms = jnp.maximum(z, 0.0) + jnp.log1p(jnp.exp(-jnp.abs(z))) - label_row * z
            part = terms[:, 0:128]
            for j in range(1, rows // 128):
                part = part + terms[:, j * 128:(j + 1) * 128]
            ebuf[me] = part
            for i, peer in enumerate(peers):
                pltpu.make_async_remote_copy(src_ref=ebuf.at[me], dst_ref=ebuf.at[me], send_sem=esend_sem, recv_sem=erecv_sem,
                                             device_id={'data': peer}, device_id_type=pl.DeviceIdType.MESH).start()
        residual = (label_row - jax.nn.sigmoid(logits)).astype(jnp.bfloat16)
        for c in range(chunks):
            cols = pl.ds(c * CHUNK, CHUNK)
            part_grad = jnp.dot(residual, feat[:, cols], preferred_element_type=jnp.float32)
            buf[par, c, me] = part_grad[:chains]
            for peer in peers:
                pltpu.make_async_remote_copy(src_ref=buf.at[par, c, me], dst_ref=buf.at[par, c, me],
                                             send_sem=send_sem.at[par, c], recv_sem=recv_sem.at[par, c],
                                             device_id={'data': peer}, device_id_type=pl.DeviceIdType.MESH).start()
        half = jnp.where(step == 0, 0.5 * step_size, step_size) if not last else 0.5 * step_size
        for c in range(chunks):
            cols = pl.ds(c * CHUNK, CHUNK)
            others = buf.at[par, c, pl.ds(0, n - 1)]
            pltpu.make_async_copy(others, others, recv_sem.at[par, c]).wait()
            grad = buf[par, c, 0]
            for k in range(1, n):
                grad = grad + buf[par, c, k]
            theta = theta_ref[:, cols]
            mom = mom_ref[:, cols] + half * (grad - theta / PRIOR_VAR)
            mom_ref[:, cols] = mom
            if not last:
                theta = theta + step_size * mom
                theta_ref[:, cols] = theta
                part = jnp.dot(lhs(theta), feat_t[cols, :], preferred_element_type=jnp.float32)
                if c == 0:
                    logits_ref[...] = part
                else:
                    logits_ref[...] = logits_ref[...] + part
        for c in range(chunks):
            others = buf.at[par, c, pl.ds(0, n - 1)]
            pltpu.make_async_copy(others, others, send_sem.at[par, c]).wait()

    def body(step, carry):
        evaluate(step, False)
        return carry

    lax.fori_loop(0, LEAPFROG, body, 0)
    evaluate(LEAPFROG, True)

    others = ebuf.at[pl.ds(0, n - 1)]
    pltpu.make_async_copy(others, others, erecv_sem).wait()
    pltpu.make_async_copy(others, others, esend_sem).wait()
    row_sum = ebuf[0]
    for k in range(1, n):
        row_sum = row_sum + ebuf[k]
    theta, mom = theta_ref[...], mom_ref[...]
    theta_out[...] = theta
    mom_out[...] = mom
    energy = (jnp.sum(row_sum, axis=1, keepdims=True) + jnp.sum(theta * theta, axis=1, keepdims=True) / (2.0 * PRIOR_VAR)
              + 0.5 * jnp.sum(mom * mom, axis=1, keepdims=True))
    energy_out[...] = jnp.broadcast_to(energy, energy_out.shape)


def solution(mesh):
    n = mesh.shape['data']

    def local_run(feat_loc, label_loc, theta_start, momentum_start):
        rows, dim = feat_loc.shape
        chains = theta_start.shape[1]
        chunks = dim // CHUNK
        step_size = STEP_COEF * math.sqrt(dim / (rows * n))
        vmem = pl.BlockSpec(memory_space=pltpu.VMEM)
        theta, mom, energy = pl.pallas_call(
            functools.partial(trajectory, n, step_size),
            out_shape=(jax.ShapeDtypeStruct((chains, dim), jnp.float32), jax.ShapeDtypeStruct((chains, dim), jnp.float32),
                       jax.ShapeDtypeStruct((chains, 128), jnp.float32)),
            in_specs=[pl.BlockSpec(memory_space=pl.ANY), vmem, vmem, vmem],
            out_specs=(vmem, vmem, vmem),
            scratch_shapes=[
                pltpu.VMEM((rows, dim), jnp.bfloat16),
                pltpu.VMEM((dim, rows), jnp.bfloat16),
                pltpu.VMEM((8, rows), jnp.float32),
                pltpu.VMEM((chains, dim), jnp.float32),
                pltpu.VMEM((chains, dim), jnp.float32),
                pltpu.VMEM((2, chunks, n, chains, CHUNK), jnp.float32),
                pltpu.VMEM((n, chains, 128), jnp.float32),
                pltpu.SemaphoreType.DMA((rows // TILE,)),
                pltpu.SemaphoreType.DMA((2, chunks)),
                pltpu.SemaphoreType.DMA((2, chunks)),
                pltpu.SemaphoreType.DMA,
                pltpu.SemaphoreType.DMA,
            ],
            compiler_params=pltpu.CompilerParams(collective_id=0, has_side_effects=True, vmem_limit_bytes=48 * 1024 * 1024),
            name='trajectory',
        )(feat_loc, label_loc[None, :], theta_start.T, momentum_start.T)
        return theta.T, mom.T, energy[:, 0]

    return jax.shard_map(local_run, mesh=mesh, in_specs=(P('data', None), P('data'), P(None, 'parts'), P(None, 'parts')),
                         out_specs=(P(None, 'parts'), P(None, 'parts'), P('parts')), check_vma=False)
```

time: 1030 us -> 174 us (0.17)
  blocking collectives: 782 us -> 0 us
  matrix products: 244 us -> 0 us
  Pallas kernels: 0 us -> 168 us
    psum x33 -> x0, blocking collectives: 782 us -> none  [grad_fn(): full_grad = lax.psum(part_grad, 'data')]
    dot_general x34 -> x0, matrix products: 244 us -> none  [the longest x33 239 us: grad_fn(): lax.dot_general(feat_loc, residual, (((0,), (0,)), ((), ())), preferred_e...]
    pallas_call x0 -> x1, Pallas kernels: none -> 168 us  [local_run(): pl.pallas_call(functools.partial(trajectory, n, step_size), out_shape=(ja...]
where the time goes in v1:
time: 174 us; the launch traced here: 172 us
  Pallas kernels  168 us (97%)
  local copies, waits for them, and re-layouts  3.93 us (2%)
    pallas_call x1, Pallas kernels, local_run(): pl.pallas_call(functools.partial(trajectory, n, step_size), out_shape=(ja...  168 us

profile of v1, /device:TPU:88, one launch (start us, length us, event | category | flops | bytes accessed | tf_op | source)
XLA Modules:
  0.0 172.3 jit_solution(11757786511565147646)
XLA Ops:
  0.6 0.0 copy-start
  0.6 0.7 copy-done
  1.3 0.0 copy-start.1
  1.3 0.7 copy-done.1
  2.0 0.0 copy-start.2
  2.0 0.7 copy-done.2
  2.7 167.8 %trajectory.1 = (f32[2,1536]{1,0:T(2,128)S(1)}, f32[2,1536]{1,0:T(2,128)S(1)}, f32[2,128]{1,0:T(2,128)S(1)}) custom-call(bf16[2048,1536]{1,0:T(8,128)(2,1)} %feat_hbm.1, s32[1,2048]{1,0:T(1,128)S(1)} %bitcast.9, f32[2,1536]{1,0:T(2,128)S(1)} %bitcast.5, f32[2,1536]{1,0:T(2,128)S(1)} %bitcast.6), custom_call_target="tpu_custom_call" | custom-call | tf_op jit(solution)/shard_map/trajectory/pallas_call | solution.py:132
  170.5 0.6 slice_reduce_fusion
  171.1 0.6 copy.9
  171.7 0.6 copy.10
Async XLA Ops:
  0.6 0.7 copy-start
  1.3 0.7 copy-start.1
  2.0 0.7 copy-start.2
